TPU v7x, 32 devices: a whole 2x2x4 slice. The times are simulated.
32 devices in a mesh: rep: 8 (over z, x), tp: 4 (over y, core).
Axes of the slice: x: 2, y: 2, z: 4, core: 2. Of those that a mesh axis runs over, the one named last changes fastest.
Arguments:
- stream_in: bfloat16 [32, 4, 8192], P('rep', None, 'tp'), may hold values from -6 to 6
- queries: bfloat16 [32, 4, 4096], P('rep'), may hold values from -90 to 90
- new_keys: bfloat16 [32, 4, 4, 128], P('rep'), may hold values from -4 to 4
- new_values: bfloat16 [32, 4, 4, 128], P('rep'), may hold values from -4 to 4
- key_cache: bfloat16 [32, 1024, 4, 128], P('rep', 'tp'), may hold values from -4.1 to 4.1
- value_cache: bfloat16 [32, 1024, 4, 128], P('rep', 'tp'), may hold values from -4 to 4
- lengths: int32 [32], P('rep'), may hold values from 2 to 1024
- out_weight: bfloat16 [4096, 8192], P('tp', 'rep'), may hold values from -0.09375 to 0.09375
- norm_gain: bfloat16 [8192], P('tp'), may hold values from 0.5 to 1.5
Outputs:
- stream_out: bfloat16 [32, 4, 8192], P('rep', None, 'tp')
- normed: bfloat16 [32, 4, 8192], P('rep', None, 'tp')
All inputs are finite; a program needn't handle non-finite values.
Results may differ from a plain program's by a relative error of at most 0.0065.
Values may be sent and summed in bfloat16 or wider, within the bound.
A program may use at most 64 MiB of HBM per device.

v0:
```python
import functools
import math

import jax
import jax.numpy as jnp
from jax import lax
from jax.experimental import pallas as pl
from jax.experimental.pallas import tpu as pltpu
from jax.sharding import PartitionSpec as P

MESH = pl.DeviceIdType.MESH
PAD = 128


def flip(index, mask, count):
    other = 0
    bit = 1
    while bit < count:
        digit = (index // bit) % 2
        other = other + bit * ((1 - digit) if mask & bit else digit)
        bit *= 2
    return other


def kernel(
    cfg,
    lengths_ref,
    q_hbm, nk_hbm, nv_hbm, k_hbm, v_hbm, w_hbm, x_hbm, gain_hbm,
    hidden_ref, scale_ref,
    q_v, k_v, v_v, w_v, x_v, gain_v,
    send_o, recv_o, send_l, recv_l,
    gathered, parts, recv_p, sq_send, sq_recv,
    load_sem, kv_sem,
    ao_send, ao_recv, al_send, al_recv, b_send, b_recv, c_send, c_recv, d_send, d_recv,
):
    n_rep, n_tp, batch, steps, heads, kv, block_len, width_all, eps = cfg
    rep = lax.axis_index("rep")
    tp = lax.axis_index("tp")
    k_own = n_rep // n_tp
    rows = batch * steps
    owned = heads // n_tp
    orow = owned * steps
    cached = block_len * kv
    fresh = steps * kv
    cw = parts.shape[2]
    hd = q_v.shape[2]
    owner = rep // k_own
    is_own = owner == tp

    sends = []
    half = batch // 2 if batch % 2 == 0 else batch
    parts_a = batch // half
    barrier = pltpu.get_barrier_semaphore()
    for j in range(1, n_tp):
        pl.semaphore_signal(barrier, inc=1, device_id=(rep, lax.rem(tp + j, n_tp)), device_id_type=MESH)
    for j in range(1, n_rep):
        pl.semaphore_signal(barrier, inc=1, device_id=(lax.rem(rep + j, n_rep), tp), device_id_type=MESH)
    for i in range(k_own):
        for t in range(n_tp):
            src_rep = tp * k_own + i

            @pl.when(jnp.logical_not((src_rep == rep) & (tp == t)))
            def _():
                pl.semaphore_signal(barrier, inc=1, device_id=(src_rep, t), device_id_type=MESH)

    loads = [pltpu.make_async_copy(q_hbm, q_v, load_sem.at[0])]
    loads[0].start()
    kv_loads = []
    for b in range(batch):
        group = [
            pltpu.make_async_copy(k_hbm.at[b], k_v.at[b, pl.ds(0, cached)], kv_sem.at[b, 0]),
            pltpu.make_async_copy(nk_hbm.at[b], k_v.at[b, pl.ds(cached, fresh)], kv_sem.at[b, 1]),
            pltpu.make_async_copy(v_hbm.at[b], v_v.at[b, pl.ds(0, cached)], kv_sem.at[b, 2]),
            pltpu.make_async_copy(nv_hbm.at[b], v_v.at[b, pl.ds(cached, fresh)], kv_sem.at[b, 3]),
        ]
        for c in group:
            c.start()
        kv_loads.append(group)
    late = [
        pltpu.make_async_copy(w_hbm, w_v, load_sem.at[1]),
        pltpu.make_async_copy(x_hbm, x_v, load_sem.at[2]),
        pltpu.make_async_copy(gain_hbm, gain_v, load_sem.at[3]),
    ]
    for c in late:
        c.start()

    for b in range(batch):
        pad = jnp.zeros((PAD - fresh, hd), jnp.bfloat16)
        k_v[b, cached + fresh : cached + PAD, :] = pad
        v_v[b, cached + fresh : cached + PAD, :] = pad

    hs = heads * steps
    cols = cached + PAD
    scaling = 1.0 / math.sqrt(hd)
    row_i = lax.broadcasted_iota(jnp.int32, (hs, cols), 0)
    col_i = lax.broadcasted_iota(jnp.int32, (hs, cols), 1)
    same = (row_i // (steps * (heads // kv))) == (col_i % kv)
    is_cached = col_i < cached
    new_t = (col_i - cached) // kv
    causal = (new_t <= row_i % steps) & (col_i < cached + fresh) & (tp == 0)
    keep = same & (is_cached | causal)
    far = jnp.int32(2**30)
    position = jnp.where(keep, jnp.where(is_cached, tp * block_len + col_i // kv, -1), far)
    lane = lax.broadcasted_iota(jnp.int32, (hs, 128), 1)
    lse = jnp.zeros((hs, 128), jnp.float32)
    loads[0].wait()
    for b in range(batch):
        for c in kv_loads[b]:
            c.wait()
        s = lax.dot_general(
            q_v[b], k_v[b], (((1,), (1,)), ((), ())), preferred_element_type=jnp.float32
        )
        s = jnp.where(position < lengths_ref[b], s * scaling, -1e30)
        top = jnp.max(s, axis=1, keepdims=True)
        p = jnp.exp(s - top)
        total = jnp.sum(p, axis=1, keepdims=True)
        num = jnp.dot(p.astype(jnp.bfloat16), v_v[b], preferred_element_type=jnp.float32)
        out = (num / total).astype(jnp.bfloat16)
        for t in range(n_tp):
            send_o[t, b] = out[t * orow : (t + 1) * orow]
        lse = jnp.where(lane == b, top + jnp.log(total), lse)
        if (b + 1) % half == 0:
            part = b // half
            if part == 0:
                arrivals = (n_tp - 1) + (n_rep - 1) + n_rep - is_own.astype(jnp.int32)
                pl.semaphore_wait(barrier, arrivals)
            if part == parts_a - 1:
                for t in range(n_tp):
                    send_l[t] = lse[t * orow : (t + 1) * orow]
            span = pl.ds(part * half, half)
            for j in range(1, n_tp):
                peer = lax.rem(tp + j, n_tp)
                if part == parts_a - 1:
                    c = pltpu.make_async_remote_copy(
                        send_l.at[peer], recv_l.at[tp], al_send.at[j], al_recv.at[tp],
                        device_id=(rep, peer), device_id_type=MESH)
                    c.start()
                    sends.append(c)
                c = pltpu.make_async_remote_copy(
                    send_o.at[peer, span], recv_o.at[tp, span], ao_send.at[part, j], ao_recv.at[part, tp],
                    device_id=(rep, peer), device_id_type=MESH)
                c.start()
                sends.append(c)

    for j in range(1, n_tp):
        peer = lax.rem(tp + j, n_tp)
        pltpu.make_async_remote_copy(
            send_l.at[peer], recv_l.at[peer], al_send.at[j], al_recv.at[peer],
            device_id=(rep, peer), device_id_type=MESH).wait_recv()
        for part in range(parts_a):
            span = pl.ds(part * half, half)
            pltpu.make_async_remote_copy(
                send_o.at[peer, span], recv_o.at[peer, span], ao_send.at[part, j], ao_recv.at[part, peer],
                device_id=(rep, peer), device_id_type=MESH).wait_recv()
    ls = [send_l[tp]] + [recv_l[lax.rem(tp + j, n_tp)] for j in range(1, n_tp)]
    os_ = [send_o[tp]] + [recv_o[lax.rem(tp + j, n_tp)] for j in range(1, n_tp)]
    most = functools.reduce(jnp.maximum, ls)
    ws = [jnp.exp(l - most) for l in ls]
    inv = 1.0 / functools.reduce(jnp.add, ws)
    ws = [w * inv for w in ws]
    att = []
    for b in range(batch):
        acc = ws[0][:, b : b + 1] * os_[0][b].astype(jnp.float32)
        for t in range(1, n_tp):
            acc = acc + ws[t][:, b : b + 1] * os_[t][b].astype(jnp.float32)
        att.append(acc.astype(jnp.bfloat16))
    att = jnp.concatenate(att, axis=0)
    m = batch * orow
    to = lax.broadcasted_iota(jnp.int32, (m, m), 0)
    frm = lax.broadcasted_iota(jnp.int32, (m, m), 1)
    want = ((to // steps) % batch) * orow + (to // rows) * steps + to % steps
    pick = jnp.where(frm == want, 1.0, 0.0).astype(jnp.bfloat16)
    att = jnp.dot(pick, att, preferred_element_type=jnp.float32).astype(jnp.bfloat16)
    gathered[rep] = jnp.concatenate([att[h * rows : (h + 1) * rows] for h in range(owned)], axis=1)

    pairs = n_rep // 2
    mid = pairs // 2
    order = [mid, *range(mid - 1, 0, -1), *range(pairs - 1, mid, -1), 0] if mid else [0]
    for mask in [m for pair in order for m in (2 * pair + 1, 2 * pair) if m]:
        peer = flip(rep, mask, n_rep)
        c = pltpu.make_async_remote_copy(
            gathered.at[rep], gathered.at[rep], b_send.at[mask], b_recv.at[rep],
            device_id=(peer, tp), device_id_type=MESH)
        c.start()
        sends.append(c)
    late[0].wait()
    slot = lax.rem(rep, k_own) * n_tp + tp
    mine = pltpu.make_async_remote_copy(
        parts.at[rep], recv_p.at[slot], c_send.at[0], c_recv.at[slot],
        device_id=(rep, owner), device_id_type=MESH)
    for pair in order:
        masks = (2 * pair + 1, 2 * pair)
        peers = [flip(rep, mask, n_rep) for mask in masks]
        for mask, peer in zip(masks, peers):
            if mask:
                pltpu.make_async_remote_copy(
                    gathered.at[peer], gathered.at[peer], b_send.at[mask], b_recv.at[peer],
                    device_id=(peer, tp), device_id_type=MESH).wait_recv()
        block = jnp.concatenate([gathered[peer] for peer in peers], axis=0)
        proj = jnp.dot(block, w_v[...], preferred_element_type=jnp.float32).astype(jnp.bfloat16)
        for i, (mask, peer) in enumerate(zip(masks, peers)):
            parts[peer] = proj[i * rows : (i + 1) * rows]
            if mask:
                c = pltpu.make_async_remote_copy(
                    parts.at[peer], recv_p.at[slot], c_send.at[mask], c_recv.at[slot],
                    device_id=(peer, owner), device_id_type=MESH)
                c.start()
                sends.append(c)

    @pl.when(is_own)
    def _():
        recv_p[slot] = parts[rep]

    @pl.when(jnp.logical_not(is_own))
    def _():
        mine.start()

    late[1].wait()
    late[2].wait()
    gain = gain_v[...].astype(jnp.float32)
    gain = jnp.concatenate([gain[c : c + 1] for c in range(gain.shape[0])], axis=1)
    x = x_v[...].astype(jnp.float32).reshape(rows, x_v.shape[2])
    for i in range(k_own):
        for t in range(n_tp):
            sid = i * n_tp + t
            src_rep = tp * k_own + i

            @pl.when(jnp.logical_not((src_rep == rep) & (tp == t)))
            def _():
                pltpu.make_async_remote_copy(
                    parts.at[0], recv_p.at[sid], c_send.at[0], c_recv.at[sid],
                    device_id=(src_rep, t), device_id_type=MESH).wait_recv()

    pieces = []
    for i in range(k_own):
        acc = recv_p[i * n_tp].astype(jnp.float32)
        for t in range(1, n_tp):
            acc = acc + recv_p[i * n_tp + t].astype(jnp.float32)
        pieces.append(acc)
    summed = jnp.concatenate(pieces, axis=1)
    hidden = x + summed
    squares = jnp.sum(hidden * hidden, axis=1, keepdims=True)

    sq_send[...] = jnp.broadcast_to(squares, sq_send.shape)
    for j in range(1, n_tp):
        peer = lax.rem(tp + j, n_tp)
        c = pltpu.make_async_remote_copy(
            sq_send, sq_recv.at[tp], d_send.at[j], d_recv.at[tp],
            device_id=(rep, peer), device_id_type=MESH)
        c.start()
        sends.append(c)
    hidden_ref[...] = hidden.reshape(hidden_ref.shape)
    every = sq_send[...]
    for j in range(1, n_tp):
        peer = lax.rem(tp + j, n_tp)
        pltpu.make_async_remote_copy(
            sq_send, sq_recv.at[peer], d_send.at[j], d_recv.at[peer],
            device_id=(rep, peer), device_id_type=MESH).wait_recv()
        every = every + sq_recv[peer]
    inverse = lax.rsqrt(every[:, :1] / width_all + eps)
    scale_ref[...] = (inverse * gain).reshape(scale_ref.shape)

    for c in sends:
        c.wait_send()

    @pl.when(jnp.logical_not(is_own))
    def _():
        mine.wait_send()


def on_device(
    n_rep, n_tp,
    stream_in, queries, new_keys, new_values, key_cache, value_cache, lengths, out_weight, norm_gain
):
    batch, steps, width = queries.shape
    block_len, kv, hd = key_cache.shape[1:]
    heads = width // hd
    depth, cw = out_weight.shape
    own_w = stream_in.shape[2]
    rows = batch * steps
    assert n_rep & (n_rep - 1) == 0
    assert n_rep % n_tp == 0 and heads % n_tp == 0
    owned = heads // n_tp
    orow = owned * steps
    hs = heads * steps
    cached = block_len * kv
    q = queries.reshape(batch, steps, heads, hd).transpose(0, 2, 1, 3).reshape(batch, hs, hd)
    nk = new_keys.reshape(batch, steps * kv, hd)
    nv = new_values.reshape(batch, steps * kv, hd)
    kc = key_cache.reshape(batch, cached, hd)
    vc = value_cache.reshape(batch, cached, hd)
    cfg = (n_rep, n_tp, batch, steps, heads, kv, block_len, own_w * n_tp, 1e-6)
    bf, f32 = jnp.bfloat16, jnp.float32
    anyspec = pl.BlockSpec(memory_space=pl.ANY)
    dma = pltpu.SemaphoreType.DMA
    hidden, scale = pl.pallas_call(
        functools.partial(kernel, cfg),
        out_shape=(
            pltpu.VMEM(stream_in.shape, f32),
            pltpu.VMEM(stream_in.shape, f32),
        ),
        in_specs=[pl.BlockSpec(memory_space=pltpu.SMEM)] + [anyspec] * 8,
        out_specs=(pl.BlockSpec(memory_space=pltpu.VMEM), pl.BlockSpec(memory_space=pltpu.VMEM)),
        scratch_shapes=[
            pltpu.VMEM((batch, hs, hd), bf),
            pltpu.VMEM((batch, cached + PAD, hd), bf),
            pltpu.VMEM((batch, cached + PAD, hd), bf),
            pltpu.VMEM((depth, cw), bf),
            pltpu.VMEM((batch, steps, own_w), bf),
            pltpu.VMEM((own_w // 128, 128), bf),
            pltpu.VMEM((n_tp, batch, orow, hd), bf),
            pltpu.VMEM((n_tp, batch, orow, hd), bf),
            pltpu.VMEM((n_tp, orow, 128), f32),
            pltpu.VMEM((n_tp, orow, 128), f32),
            pltpu.VMEM((n_rep, rows, depth), bf),
            pltpu.VMEM((n_rep, rows, cw), bf),
            pltpu.VMEM((n_rep, rows, cw), bf),
            pltpu.VMEM((rows, 128), f32),
            pltpu.VMEM((n_tp, rows, 128), f32),
            dma((4,)),
            dma((batch, 4)),
            dma((batch, n_tp)), dma((batch, n_tp)), dma((n_tp,)), dma((n_tp,)),
            dma((n_rep,)), dma((n_rep,)), dma((n_rep,)), dma((n_rep,)),
            dma((n_tp,)), dma((n_tp,)),
        ],
        compiler_params=pltpu.CompilerParams(collective_id=0, has_side_effects=True),
    )(lengths, q, nk, nv, kc, vc, out_weight, stream_in, norm_gain.reshape(own_w // 128, 128))
    return (hidden.astype(bf), (hidden * scale).astype(bf))


def solution(mesh):
    return jax.shard_map(
        functools.partial(on_device, mesh.shape["rep"], mesh.shape["tp"]),
        mesh=mesh,
        in_specs=(
            P("rep", None, "tp"),
            P("rep", None, None),
            P("rep", None, None, None),
            P("rep", None, None, None),
            P("rep", "tp", None, None),
            P("rep", "tp", None, None),
            P("rep"),
            P("tp", "rep"),
            P("tp"),
        ),
        out_specs=(P("rep", None, "tp"), P("rep", None, "tp")),
        check_vma=False,
    )
```

profile of v0, /device:TPU:0, one launch (start us, length us, event | category | flops | bytes accessed | tf_op | source)
XLA Modules:
  0.0 29.3 jit_solution(9607801668822992945)
XLA Ops:
  0.6 28.0 %shard_map.104 = (f32[4,4,2048]{2,1,0:T(4,128)S(1)}, f32[4,4,2048]{2,1,0:T(4,128)S(1)}) custom-call(s32[4]{0:T(128)} %lengths_ref.1, bf16[4,128,128]{2,1,0:T(8,128)(2,1)} %bitcast.12, bf16[4,16,128]{2,1,0:T(8,128)(2,1)} %bitcast.13, bf16[4,16,128]{2,1,0:T(8,128)(2,1)} %bitcast.14, bf16[4,1024,128]{2,1,0:T(8,128)(2,1)} %bitcast.10, ...), custom_call_target="tpu_custom_call" | custom-call | tf_op jit(solution)/shard_map/pallas_call | solution.py:296
  28.6 0.7 %multiply_convert_fusion = (bf16[4,4,2048]{2,1,0:T(4,128)(2,1)}, bf16[4,4,2048]{2,1,0:T(4,128)(2,1)}) fusion(f32[4,4,2048]{2,1,0:T(4,128)S(1)} %get-tuple-element.4, f32[4,4,2048]{2,1,0:T(4,128)S(1)} %get-tuple-element.5), kind=kLoop, calls=%fused_computation | loop fusion | flops 98304 | bytes 393216 | tf_op jit(solution)/shard_map/convert_element_type | solution.py:328
where the time goes:
time: 29.5 us; the launch traced here: 29.3 us
  Pallas kernels  28 us (95%)
  other arithmetic  0.7 us (2%)
  between operations  0.64 us (2%)
    pallas_call x1, Pallas kernels, on_device(): pl.pallas_call(functools.partial(kernel, cfg), out_shape=(pltpu.VMEM(stre...  28 us
    convert_element_type x1, other arithmetic, on_device(): return (hidden.astype(bf), (hidden * scale).astype(bf))  0.7 us

commit v1 on v0

v1 whole, which is shorter than its diff:
```python
import functools
import math

import jax
import jax.numpy as jnp
from jax import lax
from jax.experimental import pallas as pl
from jax.experimental.pallas import tpu as pltpu
from jax.sharding import PartitionSpec as P

MESH = pl.DeviceIdType.MESH
PAD = 128
LANES = 128
TILE = 8
LOADS = 5
SINGLES = 10


def flip(index, mask, count):
    other = 0
    bit = 1
    while bit < count:
        digit = (index // bit) % 2
        other = other + bit * ((1 - digit) if mask & bit else digit)
        bit *= 2
    return other


def landed(ref, sem):
    pltpu.make_async_copy(ref, ref, sem).wait()


def attend(cfg, b, length, tp, q_v, kv_v):
    n_rep, n_tp, batch, steps, heads, kv, block_len, width_all, eps = cfg
    hd = q_v.shape[2]
    group = steps * (heads // kv)
    cached = block_len * kv
    fresh = steps * kv
    chunks = cached // LANES
    scaling = 1.0 / math.sqrt(hd)
    lane = lax.broadcasted_iota(jnp.int32, (group, LANES), 1)
    row = lax.broadcasted_iota(jnp.int32, (group, LANES), 0)
    kind = lane % kv
    place = lane // kv
    causal = (place <= row % steps) & (lane < fresh) & (tp == 0)
    s = lax.dot_general(
        q_v[b], kv_v[b, 0], (((1,), (1,)), ((), ())), preferred_element_type=jnp.float32
    )
    left = length - tp * block_len
    kept = []
    for c in range(chunks + 1):
        own = s[0:group, c * LANES : (c + 1) * LANES]
        for g in range(1, kv):
            own = jnp.where(kind == g, s[g * group : (g + 1) * group, c * LANES : (c + 1) * LANES], own)
        seen = place < left - c * (LANES // kv) if c < chunks else causal
        kept.append(jnp.where(seen, own, -1e30))
    highest = functools.reduce(jnp.maximum, kept)
    tops = [jnp.max(jnp.where(kind == g, highest, -3e38), axis=1, keepdims=True) for g in range(kv)]
    top = jnp.broadcast_to(tops[0], (group, LANES))
    for g in range(1, kv):
        top = jnp.where(kind == g, tops[g], top)
    weights = [jnp.exp((k - top) * scaling) for k in kept]
    summed = functools.reduce(jnp.add, weights)
    totals = [jnp.sum(jnp.where(kind == g, summed, 0.0), axis=1, keepdims=True) for g in range(kv)]
    rounded = jnp.concatenate([w.astype(jnp.bfloat16) for w in weights], axis=1)
    one = jnp.where(kind == 0, 1.0, 0.0)
    spread = []
    for g in range(kv):
        one = jnp.where(kind == g, 1.0, 0.0).astype(jnp.bfloat16)
        spread.append(rounded * jnp.concatenate([one] * (chunks + 1), axis=1))
    spread = jnp.concatenate(spread, axis=0)
    num = jnp.dot(spread, kv_v[b, 1], preferred_element_type=jnp.float32)
    total = jnp.concatenate(totals, axis=0)
    return (num / total).astype(jnp.bfloat16), jnp.concatenate(tops, axis=0) * scaling + jnp.log(total)


def kernel(
    cfg, order, far,
    len_hbm, q_hbm, nk_hbm, nv_hbm, k_hbm, v_hbm, w_hbm, x_hbm, gain_hbm,
    hidden_ref, scale_ref,
    len_s, q_v, kv_v, w_v, gain_v,
    send_o, recv_o, send_l, recv_l, mix,
    gathered, parts, other, ready, recv_c, x_v, sq_s, sq_r,
    sems,
):
    n_rep, n_tp, batch, steps, heads, kv, block_len, width_all, eps = cfg
    rep = lax.axis_index("rep")
    tp = lax.axis_index("tp")
    k_own = n_rep // n_tp
    pairs = n_rep // 2
    rows = batch * steps
    owned = heads // n_tp
    orow = owned * steps
    hs = heads * steps
    cached = block_len * kv
    fresh = steps * kv
    cw = w_v.shape[1]
    hd = q_v.shape[2]
    owner = rep // k_own
    core = lax.rem(tp, 2)
    chips = n_tp // 2
    is_own = (owner == tp) & (lax.rem(rep, 2) == core)
    not_own = jnp.logical_not(is_own)
    slot = lax.rem(rep, k_own) * chips + tp // 2

    s_len, s_q, s_w, s_gain, s_x = (sems.at[i] for i in range(LOADS))
    s_kv = [sems.at[LOADS + b] for b in range(batch)]
    first = LOADS + batch
    (ao_s, ao_r, al_s, al_r, b_s, d_s, c_s, c_r, q_s, q_r) = (
        sems.at[first + i] for i in range(SINGLES)
    )
    first += SINGLES
    b_r = [sems.at[first + p] for p in range(pairs)]
    d_r = [sems.at[first + pairs + p] for p in range(pairs)]

    loads = [pltpu.make_async_copy(q_hbm, q_v, s_q)]
    for b in range(batch):
        loads += [
            pltpu.make_async_copy(k_hbm.at[b], kv_v.at[b, 0, pl.ds(0, cached)], s_kv[b]),
            pltpu.make_async_copy(nk_hbm.at[b], kv_v.at[b, 0, pl.ds(cached, fresh)], s_kv[b]),
            pltpu.make_async_copy(v_hbm.at[b], kv_v.at[b, 1, pl.ds(0, cached)], s_kv[b]),
            pltpu.make_async_copy(nv_hbm.at[b], kv_v.at[b, 1, pl.ds(cached, fresh)], s_kv[b]),
        ]
        if b == 0:
            loads.append(pltpu.make_async_copy(len_hbm, len_s, s_len))
    loads += [
        pltpu.make_async_copy(w_hbm, w_v, s_w),
        pltpu.make_async_copy(gain_hbm, gain_v, s_gain),
        pltpu.make_async_copy(x_hbm, x_v, s_x),
    ]
    for c in loads:
        c.start()

    barrier = pltpu.get_barrier_semaphore()
    for j in range(n_rep - 1, 0, -1):
        pl.semaphore_signal(barrier, inc=1, device_id=(lax.rem(rep + j, n_rep), tp), device_id_type=MESH)
    for j in range(1, n_tp):
        pl.semaphore_signal(barrier, inc=1, device_id=(rep, lax.rem(tp + j, n_tp)), device_id_type=MESH)
    for i in range(k_own):
        for h in range(chips):
            source = (tp * k_own + i, 2 * h + lax.rem(rep, 2))
            mine = (source[0] == rep) & (source[1] == tp)

            @pl.when(jnp.logical_not(mine))
            def _():
                pl.semaphore_signal(barrier, inc=1, device_id=source, device_id_type=MESH)

    for b in range(batch):
        for i in range(2):
            kv_v[b, i, cached + fresh : cached + PAD, :] = jnp.zeros((PAD - fresh, hd), jnp.bfloat16)

    lane = lax.broadcasted_iota(jnp.int32, (hs, LANES), 1)
    lse = jnp.zeros((hs, LANES), jnp.float32)
    landed(len_s, s_len)
    landed(q_v, s_q)
    together = 2 if batch % 2 == 0 else 1
    for b0 in range(0, batch, together):
        for b in range(b0, b0 + together):
            landed(kv_v.at[b, :, pl.ds(0, cached + fresh)], s_kv[b])
        for b in range(b0, b0 + together):
            out, value = attend(cfg, b, len_s[b], tp, q_v, kv_v)
            for t in range(n_tp):
                send_o[t, b] = out[t * orow : (t + 1) * orow]
            lse = jnp.where(lane == b, value, lse)
    send_l[...] = lse.T[:TILE]

    pl.semaphore_wait(barrier, (n_tp - 1) + (n_rep - 1) + n_rep // 2 - is_own.astype(jnp.int32))
    for j in range(1, n_tp):
        peer = lax.rem(tp + j, n_tp)
        pltpu.make_async_remote_copy(
            send_l, recv_l.at[j - 1], al_s, al_r, device_id=(rep, peer), device_id_type=MESH).start()
        pltpu.make_async_remote_copy(
            send_o.at[peer], recv_o.at[j - 1], ao_s, ao_r, device_id=(rep, peer), device_id_type=MESH).start()

    landed(recv_l, al_r)
    ls = [send_l[...]] + [recv_l[j] for j in range(n_tp - 1)]
    most = functools.reduce(jnp.maximum, ls)
    ws = [jnp.exp(l - most) for l in ls]
    inv = 1.0 / functools.reduce(jnp.add, ws)
    ws = [w * inv for w in ws]
    if n_tp * TILE < LANES:
        ws.append(jnp.zeros((LANES - n_tp * TILE, hs), jnp.float32))
    mix[...] = jnp.concatenate(ws, axis=0).T
    share = mix[pl.ds(pl.multiple_of(tp * orow, orow), orow), :]
    landed(recv_o, ao_r)
    att = []
    for b in range(batch):
        acc = share[:, b : b + 1] * send_o[tp, b].astype(jnp.float32)
        for j in range(1, n_tp):
            acc = acc + share[:, j * TILE + b : j * TILE + b + 1] * recv_o[j - 1, b].astype(jnp.float32)
        att.append(acc.astype(jnp.bfloat16))
    att = jnp.concatenate(att, axis=0)
    m = batch * orow
    to = lax.broadcasted_iota(jnp.int32, (m, m), 0)
    frm = lax.broadcasted_iota(jnp.int32, (m, m), 1)
    want = ((to // steps) % batch) * orow + (to // rows) * steps + to % steps
    pick = jnp.where(frm == want, 1.0, 0.0).astype(jnp.bfloat16)
    att = jnp.dot(pick, att, preferred_element_type=jnp.float32).astype(jnp.bfloat16)
    gathered[rep] = jnp.concatenate([att[h * rows : (h + 1) * rows] for h in range(owned)], axis=1)

    for mask in far:
        pltpu.make_async_remote_copy(
            gathered.at[rep], gathered.at[rep], b_s, sems.at[first + rep // 2],
            device_id=(flip(rep, mask, n_rep), tp), device_id_type=MESH).start()
    partner = tp + 1 - 2 * core

    def pass_on(p):
        landed(other.at[p], d_r[p])
        both = parts[p, core].astype(jnp.float32) + other[p].astype(jnp.float32)
        ready[p] = both.astype(jnp.bfloat16)
        local = is_own & (rep // 2 == p)

        @pl.when(jnp.logical_not(local))
        def _():
            pltpu.make_async_remote_copy(
                ready.at[p], recv_c.at[slot], c_s, c_r,
                device_id=(2 * p + core, owner), device_id_type=MESH).start()

        @pl.when(local)
        def _():
            recv_c[slot] = ready[p]

    landed(w_v, s_w)
    waiting = []
    for batch_of in order:
        for p in batch_of:
            mine = rep // 2 == p

            @pl.when(mine)
            def _():
                landed(gathered.at[0], b_r[p])

            @pl.when(jnp.logical_not(mine))
            def _():
                landed(gathered.at[pl.ds(2 * p, 2)], b_r[p])

        block = jnp.concatenate([gathered[2 * p + i] for p in batch_of for i in range(2)], axis=0)
        proj = jnp.dot(block, w_v[...], preferred_element_type=jnp.float32).astype(jnp.bfloat16)
        for n, p in enumerate(batch_of):
            for i in range(2):
                parts[p, i] = proj[(2 * n + i) * rows : (2 * n + i + 1) * rows]
            pltpu.make_async_remote_copy(
                parts.at[p, 1 - core], other.at[p], d_s, d_r[p],
                device_id=(rep, partner), device_id_type=MESH).start()
        for p in waiting:
            pass_on(p)
        waiting = batch_of
    for p in waiting:
        pass_on(p)

    landed(x_v, s_x)
    landed(gain_v, s_gain)
    gain = gain_v[...].astype(jnp.float32)
    gain = jnp.concatenate([gain[c : c + 1] for c in range(gain.shape[0])], axis=1)

    x = x_v[...].astype(jnp.float32).reshape(rows, x_v.shape[2])
    spot = lax.broadcasted_iota(jnp.int32, (rows, LANES), 0) == lax.broadcasted_iota(jnp.int32, (rows, LANES), 1)

    @pl.when(is_own)
    def _():
        landed(recv_c.at[pl.ds(0, n_rep // 2 - 1)], c_r)

    @pl.when(not_own)
    def _():
        landed(recv_c, c_r)

    pieces = []
    for i in range(k_own):
        acc = recv_c[i * chips].astype(jnp.float32)
        for h in range(1, chips):
            acc = acc + recv_c[i * chips + h].astype(jnp.float32)
        pieces.append(acc)
    hidden = x + jnp.concatenate(pieces, axis=1)
    squares = jnp.sum(hidden * hidden, axis=1, keepdims=True)
    sq_s[...] = jnp.sum(jnp.where(spot, squares, 0.0), axis=0, keepdims=True)
    for j in range(1, n_tp):
        pltpu.make_async_remote_copy(
            sq_s, sq_r.at[pl.ds(j, 1)], q_s, q_r,
            device_id=(rep, lax.rem(tp + j, n_tp)), device_id_type=MESH).start()
    sq_r[0:1, :] = sq_s[...]
    hidden_ref[...] = hidden.reshape(hidden_ref.shape)
    landed(sq_r.at[pl.ds(1, n_tp - 1)], q_r)
    every = jnp.sum(sq_r[...], axis=0, keepdims=True)
    every = jnp.sum(jnp.where(spot, every, 0.0), axis=1, keepdims=True)
    inverse = lax.rsqrt(every / width_all + eps)
    scale_ref[...] = (inverse * gain).reshape(scale_ref.shape)

    landed(recv_l, al_s)
    landed(recv_o, ao_s)
    landed(gathered.at[pl.ds(1, n_rep - 1)], b_s)
    landed(other, d_s)
    landed(sq_r.at[pl.ds(1, n_tp - 1)], q_s)

    @pl.when(is_own)
    def _():
        landed(ready.at[pl.ds(0, pairs - 1)], c_s)

    @pl.when(not_own)
    def _():
        landed(ready, c_s)


def on_device(
    n_rep, n_tp,
    stream_in, queries, new_keys, new_values, key_cache, value_cache, lengths, out_weight, norm_gain
):
    batch, steps, width = queries.shape
    block_len, kv, hd = key_cache.shape[1:]
    heads = width // hd
    depth, cw = out_weight.shape
    own_w = stream_in.shape[2]
    rows = batch * steps
    k_own = n_rep // n_tp
    assert n_rep & (n_rep - 1) == 0
    assert n_rep % n_tp == 0 and k_own % 2 == 0 and n_tp % 2 == 0 and heads % n_tp == 0
    assert batch <= TILE and k_own <= TILE and rows <= LANES and n_tp * TILE <= LANES
    owned = heads // n_tp
    orow = owned * steps
    hs = heads * steps
    cached = block_len * kv
    assert cached % LANES == 0 and LANES % kv == 0 and steps * kv <= PAD and hs % LANES == 0
    q = queries.reshape(batch, steps, heads, hd).transpose(0, 2, 1, 3).reshape(batch, hs, hd)
    nk = new_keys.reshape(batch, steps * kv, hd)
    nv = new_values.reshape(batch, steps * kv, hd)
    kc = key_cache.reshape(batch, cached, hd)
    vc = value_cache.reshape(batch, cached, hd)
    cfg = (n_rep, n_tp, batch, steps, heads, kv, block_len, own_w * n_tp, 1e-6)
    pairs = n_rep // 2
    order = [[0], [1], [2, 3]] if pairs == 4 else [[p] for p in range(pairs)]
    far = [m for p in range(pairs - 1, -1, -1) for m in (2 * p + 1, 2 * p) if m]
    bf, f32 = jnp.bfloat16, jnp.float32
    anyspec = pl.BlockSpec(memory_space=pl.ANY)
    vmem = pl.BlockSpec(memory_space=pltpu.VMEM)
    hidden, scale = pl.pallas_call(
        functools.partial(kernel, cfg, order, far),
        out_shape=(
            pltpu.VMEM(stream_in.shape, f32),
            pltpu.VMEM(stream_in.shape, f32),
        ),
        in_specs=[anyspec] * 9,
        out_specs=(vmem, vmem),
        scratch_shapes=[
            pltpu.SMEM((batch,), jnp.int32),
            pltpu.VMEM((batch, hs, hd), bf),
            pltpu.VMEM((batch, 2, cached + PAD, hd), bf),
            pltpu.VMEM((depth, cw), bf),
            pltpu.VMEM((own_w // 128, 128), bf),
            pltpu.VMEM((n_tp, batch, orow, hd), bf),
            pltpu.VMEM((n_tp - 1, batch, orow, hd), bf),
            pltpu.VMEM((TILE, hs), f32),
            pltpu.VMEM((n_tp - 1, TILE, hs), f32),
            pltpu.VMEM((hs, LANES), f32),
            pltpu.VMEM((n_rep, rows, depth), bf),
            pltpu.VMEM((pairs, 2, rows, cw), bf),
            pltpu.VMEM((pairs, rows, cw), bf),
            pltpu.VMEM((pairs, rows, cw), bf),
            pltpu.VMEM((n_rep // 2, rows, cw), bf),
            pltpu.VMEM((batch, steps, own_w), bf),
            pltpu.VMEM((1, LANES), f32),
            pltpu.VMEM((n_tp, LANES), f32),
            pltpu.SemaphoreType.DMA((LOADS + batch + SINGLES + 2 * pairs,)),
        ],
        compiler_params=pltpu.CompilerParams(collective_id=0, has_side_effects=True),
    )(lengths, q, nk, nv, kc, vc, out_weight, stream_in, norm_gain.reshape(own_w // 128, 128))
    return (hidden.astype(bf), (hidden * scale).astype(bf))


def solution(mesh):
    return jax.shard_map(
        functools.partial(on_device, mesh.shape["rep"], mesh.shape["tp"]),
        mesh=mesh,
        in_specs=(
            P("rep", None, "tp"),
            P("rep", None, None),
            P("rep", None, None, None),
            P("rep", None, None, None),
            P("rep", "tp", None, None),
            P("rep", "tp", None, None),
            P("rep"),
            P("tp", "rep"),
            P("tp"),
        ),
        out_specs=(P("rep", None, "tp"), P("rep", None, "tp")),
        check_vma=False,
    )
```

time: 29.5 us -> 26.7 us (0.905)
  Pallas kernels: 28 us -> 25.2 us
    pallas_call x1, Pallas kernels: 28 us -> 25.2 us  [on_device(): pl.pallas_call(functools.partial(kernel, cfg, order, far), out_shape=(plt...]
where the time goes in v1:
time: 26.7 us; the launch traced here: 26.5 us
  Pallas kernels  25.2 us (94%)
  other arithmetic  0.7 us (3%)
  between operations  0.64 us (2%)
    pallas_call x1, Pallas kernels, on_device(): pl.pallas_call(functools.partial(kernel, cfg, order, far), out_shape=(plt...  25.2 us
    convert_element_type x1, other arithmetic, on_device(): return (hidden.astype(bf), (hidden * scale).astype(bf))  0.7 us

profile of v1, /device:TPU:0, one launch (start us, length us, event | category | flops | bytes accessed | tf_op | source)
XLA Modules:
  0.0 26.5 jit_solution(1919872823222855038)
XLA Ops:
  0.6 25.2 %shard_map.104 = (f32[4,4,2048]{2,1,0:T(4,128)S(1)}, f32[4,4,2048]{2,1,0:T(4,128)S(1)}) custom-call(s32[4]{0:T(128)} %len_hbm.1, bf16[4,128,128]{2,1,0:T(8,128)(2,1)} %bitcast.12, bf16[4,16,128]{2,1,0:T(8,128)(2,1)} %bitcast.13, bf16[4,16,128]{2,1,0:T(8,128)(2,1)} %bitcast.14, bf16[4,1024,128]{2,1,0:T(8,128)(2,1)} %bitcast.10, ...), custom_call_target="tpu_custom_call" | custom-call | tf_op jit(solution)/shard_map/pallas_call | solution.py:334
  25.8 0.7 %multiply_convert_fusion = (bf16[4,4,2048]{2,1,0:T(4,128)(2,1)}, bf16[4,4,2048]{2,1,0:T(4,128)(2,1)}) fusion(f32[4,4,2048]{2,1,0:T(4,128)S(1)} %get-tuple-element.4, f32[4,4,2048]{2,1,0:T(4,128)S(1)} %get-tuple-element.5), kind=kLoop, calls=%fused_computation | loop fusion | flops 98304 | bytes 393216 | tf_op jit(solution)/shard_map/convert_element_type | solution.py:365

commit v2 on v1

--- a/solution.py
+++ b/solution.py
@@ -11,6 +11,7 @@
 MESH = pl.DeviceIdType.MESH
 PAD = 128
 LANES = 128
+LEAD = 1
 TILE = 8
 LOADS = 5
 SINGLES = 10
@@ -81,7 +82,7 @@
     len_s, q_v, kv_v, w_v, gain_v,
     send_o, recv_o, send_l, recv_l, mix,
     gathered, parts, other, ready, recv_c, x_v, sq_s, sq_r,
-    sems,
+    sems, news,
 ):
     n_rep, n_tp, batch, steps, heads, kv, block_len, width_all, eps = cfg
     rep = lax.axis_index("rep")
@@ -99,7 +100,9 @@
     owner = rep // k_own
     core = lax.rem(tp, 2)
     chips = n_tp // 2
-    is_own = (owner == tp) & (lax.rem(rep, 2) == core)
+    line = rep // 2
+    half = pairs // 2
+    is_own = (owner == tp) & (core == 0)
     not_own = jnp.logical_not(is_own)
     slot = lax.rem(rep, k_own) * chips + tp // 2
 
@@ -132,18 +135,24 @@
         c.start()
 
     barrier = pltpu.get_barrier_semaphore()
+    leads = tp == LEAD
+
+    def greet(group):
+        pl.semaphore_signal(barrier, inc=1, device_id=(group, LEAD), device_id_type=MESH)
+
     for j in range(n_rep - 1, 0, -1):
-        pl.semaphore_signal(barrier, inc=1, device_id=(lax.rem(rep + j, n_rep), tp), device_id_type=MESH)
+        greet(lax.rem(rep + j, n_rep))
+
+    @pl.when(jnp.logical_not(leads))
+    def _():
+        greet(rep)
+
     for j in range(1, n_tp):
-        pl.semaphore_signal(barrier, inc=1, device_id=(rep, lax.rem(tp + j, n_tp)), device_id_type=MESH)
-    for i in range(k_own):
-        for h in range(chips):
-            source = (tp * k_own + i, 2 * h + lax.rem(rep, 2))
-            mine = (source[0] == rep) & (source[1] == tp)
-
-            @pl.when(jnp.logical_not(mine))
-            def _():
-                pl.semaphore_signal(barrier, inc=1, device_id=source, device_id_type=MESH)
+        peer = lax.rem(tp + j, n_tp)
+
+        @pl.when(peer != LEAD)
+        def _():
+            pl.semaphore_signal(barrier, inc=1, device_id=(rep, peer), device_id_type=MESH)
 
     for b in range(batch):
         for i in range(2):
@@ -153,7 +162,7 @@
     lse = jnp.zeros((hs, LANES), jnp.float32)
     landed(len_s, s_len)
     landed(q_v, s_q)
-    together = 2 if batch % 2 == 0 else 1
+    together = 1
     for b0 in range(0, batch, together):
         for b in range(b0, b0 + together):
             landed(kv_v.at[b, :, pl.ds(0, cached + fresh)], s_kv[b])
@@ -162,15 +171,29 @@
             for t in range(n_tp):
                 send_o[t, b] = out[t * orow : (t + 1) * orow]
             lse = jnp.where(lane == b, value, lse)
+        if b0 == 0:
+            @pl.when(jnp.logical_not(leads))
+            def _():
+                pl.semaphore_wait(barrier, n_tp - 1)
+                pl.semaphore_signal(news, inc=1, device_id=(rep, LEAD), device_id_type=MESH)
     send_l[...] = lse.T[:TILE]
 
-    pl.semaphore_wait(barrier, (n_tp - 1) + (n_rep - 1) + n_rep // 2 - is_own.astype(jnp.int32))
+    @pl.when(leads)
+    def _():
+        pl.semaphore_wait(news, n_tp - 1)
+
     for j in range(1, n_tp):
         peer = lax.rem(tp + j, n_tp)
         pltpu.make_async_remote_copy(
             send_l, recv_l.at[j - 1], al_s, al_r, device_id=(rep, peer), device_id_type=MESH).start()
         pltpu.make_async_remote_copy(
             send_o.at[peer], recv_o.at[j - 1], ao_s, ao_r, device_id=(rep, peer), device_id_type=MESH).start()
+
+    @pl.when(leads)
+    def _():
+        pl.semaphore_wait(barrier, n_rep * n_tp - 1)
+        for j in range(1, n_tp):
+            pl.semaphore_signal(news, inc=1, device_id=(rep, lax.rem(tp + j, n_tp)), device_id_type=MESH)
 
     landed(recv_l, al_r)
     ls = [send_l[...]] + [recv_l[j] for j in range(n_tp - 1)]
@@ -198,31 +221,44 @@
     att = jnp.dot(pick, att, preferred_element_type=jnp.float32).astype(jnp.bfloat16)
     gathered[rep] = jnp.concatenate([att[h * rows : (h + 1) * rows] for h in range(owned)], axis=1)
 
+    @pl.when(jnp.logical_not(leads))
+    def _():
+        pl.semaphore_wait(news, 1)
+
     for mask in far:
         pltpu.make_async_remote_copy(
             gathered.at[rep], gathered.at[rep], b_s, sems.at[first + rep // 2],
             device_id=(flip(rep, mask, n_rep), tp), device_id_type=MESH).start()
     partner = tp + 1 - 2 * core
 
-    def pass_on(p):
-        landed(other.at[p], d_r[p])
-        both = parts[p, core].astype(jnp.float32) + other[p].astype(jnp.float32)
-        ready[p] = both.astype(jnp.bfloat16)
-        local = is_own & (rep // 2 == p)
-
-        @pl.when(jnp.logical_not(local))
+    def keeper(p):
+        return ((line < half) if p >= half else (line >= half)).astype(jnp.int32)
+
+    def pass_on(p, when):
+        @pl.when(when & (core == keeper(p)))
         def _():
-            pltpu.make_async_remote_copy(
-                ready.at[p], recv_c.at[slot], c_s, c_r,
-                device_id=(2 * p + core, owner), device_id_type=MESH).start()
-
-        @pl.when(local)
-        def _():
-            recv_c[slot] = ready[p]
+            landed(other.at[p], d_r[p])
+            for i in range(2):
+                both = parts[p, i].astype(jnp.float32) + other[p, i].astype(jnp.float32)
+                ready[p, i] = both.astype(jnp.bfloat16)
+                local = is_own & (rep == 2 * p + i)
+
+                @pl.when(jnp.logical_not(local))
+                def _():
+                    pltpu.make_async_remote_copy(
+                        ready.at[p, i], recv_c.at[slot], c_s, c_r,
+                        device_id=(2 * p + i, owner), device_id_type=MESH).start()
+
+                @pl.when(local)
+                def _():
+                    recv_c[slot] = ready[p, i]
 
     landed(w_v, s_w)
     waiting = []
     for batch_of in order:
+        distant = functools.reduce(jnp.logical_or, [jnp.abs(line - p) > 1 for p in batch_of])
+        for p in waiting:
+            pass_on(p, distant)
         for p in batch_of:
             mine = rep // 2 == p
 
@@ -239,14 +275,17 @@
         for n, p in enumerate(batch_of):
             for i in range(2):
                 parts[p, i] = proj[(2 * n + i) * rows : (2 * n + i + 1) * rows]
-            pltpu.make_async_remote_copy(
-                parts.at[p, 1 - core], other.at[p], d_s, d_r[p],
-                device_id=(rep, partner), device_id_type=MESH).start()
+            @pl.when(core != keeper(p))
+            def _():
+                pltpu.make_async_remote_copy(
+                    parts.at[p], other.at[p], d_s, d_r[p],
+                    device_id=(rep, partner), device_id_type=MESH).start()
+
         for p in waiting:
-            pass_on(p)
+            pass_on(p, jnp.logical_not(distant))
         waiting = batch_of
     for p in waiting:
-        pass_on(p)
+        pass_on(p, line >= 0)
 
     landed(x_v, s_x)
     landed(gain_v, s_gain)
@@ -288,16 +327,16 @@
     landed(recv_l, al_s)
     landed(recv_o, ao_s)
     landed(gathered.at[pl.ds(1, n_rep - 1)], b_s)
-    landed(other, d_s)
+    landed(other.at[pl.ds(0, half)], d_s)
     landed(sq_r.at[pl.ds(1, n_tp - 1)], q_s)
 
     @pl.when(is_own)
     def _():
-        landed(ready.at[pl.ds(0, pairs - 1)], c_s)
+        landed(recv_c.at[pl.ds(0, n_rep // 2 - 1)], c_s)
 
     @pl.when(not_own)
     def _():
-        landed(ready, c_s)
+        landed(recv_c, c_s)
 
 
 def on_device(
@@ -352,13 +391,14 @@
             pltpu.VMEM((hs, LANES), f32),
             pltpu.VMEM((n_rep, rows, depth), bf),
             pltpu.VMEM((pairs, 2, rows, cw), bf),
-            pltpu.VMEM((pairs, rows, cw), bf),
-            pltpu.VMEM((pairs, rows, cw), bf),
+            pltpu.VMEM((pairs, 2, rows, cw), bf),
+            pltpu.VMEM((pairs, 2, rows, cw), bf),
             pltpu.VMEM((n_rep // 2, rows, cw), bf),
             pltpu.VMEM((batch, steps, own_w), bf),
             pltpu.VMEM((1, LANES), f32),
             pltpu.VMEM((n_tp, LANES), f32),
             pltpu.SemaphoreType.DMA((LOADS + batch + SINGLES + 2 * pairs,)),
+            pltpu.SemaphoreType.REGULAR,
         ],
         compiler_params=pltpu.CompilerParams(collective_id=0, has_side_effects=True),
     )(lengths, q, nk, nv, kc, vc, out_weight, stream_in, norm_gain.reshape(own_w // 128, 128))

time: 26.7 us -> 25.4 us (0.951)
  Pallas kernels: 25.2 us -> 23.7 us
    pallas_call x1, Pallas kernels: 25.2 us -> 23.7 us  [on_device(): pl.pallas_call(functools.partial(kernel, cfg, order, far), out_shape=(plt...]
where the time goes in v2:
time: 25.4 us; the launch traced here: 25.1 us
  Pallas kernels  23.7 us (93%)
  other arithmetic  0.7 us (3%)
  between operations  0.64 us (3%)
    pallas_call x1, Pallas kernels, on_device(): pl.pallas_call(functools.partial(kernel, cfg, order, far), out_shape=(plt...  23.7 us
    convert_element_type x1, other arithmetic, on_device(): return (hidden.astype(bf), (hidden * scale).astype(bf))  0.7 us

profile of v2, /device:TPU:0, one launch (start us, length us, event | category | flops | bytes accessed | tf_op | source)
XLA Modules:
  0.0 25.1 jit_solution(2245441876913220281)
XLA Ops:
  0.6 23.7 %shard_map.104 = (f32[4,4,2048]{2,1,0:T(4,128)S(1)}, f32[4,4,2048]{2,1,0:T(4,128)S(1)}) custom-call(s32[4]{0:T(128)} %len_hbm.1, bf16[4,128,128]{2,1,0:T(8,128)(2,1)} %bitcast.12, bf16[4,16,128]{2,1,0:T(8,128)(2,1)} %bitcast.13, bf16[4,16,128]{2,1,0:T(8,128)(2,1)} %bitcast.14, bf16[4,1024,128]{2,1,0:T(8,128)(2,1)} %bitcast.10, ...), custom_call_target="tpu_custom_call" | custom-call | tf_op jit(solution)/shard_map/pallas_call | solution.py:373
  24.4 0.7 %multiply_convert_fusion = (bf16[4,4,2048]{2,1,0:T(4,128)(2,1)}, bf16[4,4,2048]{2,1,0:T(4,128)(2,1)}) fusion(f32[4,4,2048]{2,1,0:T(4,128)S(1)} %get-tuple-element.4, f32[4,4,2048]{2,1,0:T(4,128)S(1)} %get-tuple-element.5), kind=kLoop, calls=%fused_computation | loop fusion | flops 98304 | bytes 393216 | tf_op jit(solution)/shard_map/convert_element_type | solution.py:405

commit v3 on v2

--- a/solution.py
+++ b/solution.py
@@ -31,19 +31,19 @@
     pltpu.make_async_copy(ref, ref, sem).wait()
 
 
-def attend(cfg, b, length, tp, q_v, kv_v):
+def lanes_of(cfg):
     n_rep, n_tp, batch, steps, heads, kv, block_len, width_all, eps = cfg
-    hd = q_v.shape[2]
     group = steps * (heads // kv)
-    cached = block_len * kv
-    fresh = steps * kv
-    chunks = cached // LANES
-    scaling = 1.0 / math.sqrt(hd)
     lane = lax.broadcasted_iota(jnp.int32, (group, LANES), 1)
     row = lax.broadcasted_iota(jnp.int32, (group, LANES), 0)
-    kind = lane % kv
-    place = lane // kv
-    causal = (place <= row % steps) & (lane < fresh) & (tp == 0)
+    return group, lane, row, lane % kv, lane // kv
+
+
+def score(cfg, b, length, tp, q_v, kv_v):
+    n_rep, n_tp, batch, steps, heads, kv, block_len, width_all, eps = cfg
+    group, lane, row, kind, place = lanes_of(cfg)
+    chunks = block_len * kv // LANES
+    causal = (place <= row % steps) & (lane < steps * kv) & (tp == 0)
     s = lax.dot_general(
         q_v[b], kv_v[b, 0], (((1,), (1,)), ((), ())), preferred_element_type=jnp.float32
     )
@@ -55,6 +55,12 @@
             own = jnp.where(kind == g, s[g * group : (g + 1) * group, c * LANES : (c + 1) * LANES], own)
         seen = place < left - c * (LANES // kv) if c < chunks else causal
         kept.append(jnp.where(seen, own, -1e30))
+    return kept
+
+
+def soften(cfg, kept, scaling):
+    kv = cfg[5]
+    group, lane, row, kind, place = lanes_of(cfg)
     highest = functools.reduce(jnp.maximum, kept)
     tops = [jnp.max(jnp.where(kind == g, highest, -3e38), axis=1, keepdims=True) for g in range(kv)]
     top = jnp.broadcast_to(tops[0], (group, LANES))
@@ -63,16 +69,19 @@
     weights = [jnp.exp((k - top) * scaling) for k in kept]
     summed = functools.reduce(jnp.add, weights)
     totals = [jnp.sum(jnp.where(kind == g, summed, 0.0), axis=1, keepdims=True) for g in range(kv)]
-    rounded = jnp.concatenate([w.astype(jnp.bfloat16) for w in weights], axis=1)
-    one = jnp.where(kind == 0, 1.0, 0.0)
+    rounded = [w.astype(jnp.bfloat16) for w in weights]
+    return rounded, jnp.concatenate(tops, axis=0), jnp.concatenate(totals, axis=0)
+
+
+def blend(cfg, rounded, values):
+    kv = cfg[5]
+    group, lane, row, kind, place = lanes_of(cfg)
     spread = []
     for g in range(kv):
         one = jnp.where(kind == g, 1.0, 0.0).astype(jnp.bfloat16)
-        spread.append(rounded * jnp.concatenate([one] * (chunks + 1), axis=1))
+        spread.append(jnp.concatenate([w * one for w in rounded], axis=1))
     spread = jnp.concatenate(spread, axis=0)
-    num = jnp.dot(spread, kv_v[b, 1], preferred_element_type=jnp.float32)
-    total = jnp.concatenate(totals, axis=0)
-    return (num / total).astype(jnp.bfloat16), jnp.concatenate(tops, axis=0) * scaling + jnp.log(total)
+    return jnp.dot(spread, values, preferred_element_type=jnp.float32)
 
 
 def kernel(
@@ -108,23 +117,25 @@
 
     s_len, s_q, s_w, s_gain, s_x = (sems.at[i] for i in range(LOADS))
     s_kv = [sems.at[LOADS + b] for b in range(batch)]
-    first = LOADS + batch
+    s_vv = [sems.at[LOADS + batch + b] for b in range(batch)]
+    first = LOADS + 2 * batch
     (ao_s, ao_r, al_s, al_r, b_s, d_s, c_s, c_r, q_s, q_r) = (
         sems.at[first + i] for i in range(SINGLES)
     )
     first += SINGLES
     b_r = [sems.at[first + p] for p in range(pairs)]
     d_r = [sems.at[first + pairs + p] for p in range(pairs)]
+    z_r = [sems.at[first + 2 * pairs + p] for p in range(pairs)]
 
     loads = [pltpu.make_async_copy(q_hbm, q_v, s_q)]
-    for b in range(batch):
-        loads += [
-            pltpu.make_async_copy(k_hbm.at[b], kv_v.at[b, 0, pl.ds(0, cached)], s_kv[b]),
-            pltpu.make_async_copy(nk_hbm.at[b], kv_v.at[b, 0, pl.ds(cached, fresh)], s_kv[b]),
-            pltpu.make_async_copy(v_hbm.at[b], kv_v.at[b, 1, pl.ds(0, cached)], s_kv[b]),
-            pltpu.make_async_copy(nv_hbm.at[b], kv_v.at[b, 1, pl.ds(cached, fresh)], s_kv[b]),
-        ]
-        if b == 0:
+    for b0 in range(0, batch, batch):
+        for i, old, new, marks in ((0, k_hbm, nk_hbm, s_kv), (1, v_hbm, nv_hbm, s_vv)):
+            for b in range(b0, b0 + batch):
+                loads += [
+                    pltpu.make_async_copy(old.at[b], kv_v.at[b, i, pl.ds(0, cached)], marks[b]),
+                    pltpu.make_async_copy(new.at[b], kv_v.at[b, i, pl.ds(cached, fresh)], marks[b]),
+                ]
+        if b0 == 0:
             loads.append(pltpu.make_async_copy(len_hbm, len_s, s_len))
     loads += [
         pltpu.make_async_copy(w_hbm, w_v, s_w),
@@ -162,20 +173,29 @@
     lse = jnp.zeros((hs, LANES), jnp.float32)
     landed(len_s, s_len)
     landed(q_v, s_q)
-    together = 1
+    scaling = 1.0 / math.sqrt(hd)
+    together = batch
     for b0 in range(0, batch, together):
-        for b in range(b0, b0 + together):
-            landed(kv_v.at[b, :, pl.ds(0, cached + fresh)], s_kv[b])
-        for b in range(b0, b0 + together):
-            out, value = attend(cfg, b, len_s[b], tp, q_v, kv_v)
-            for t in range(n_tp):
-                send_o[t, b] = out[t * orow : (t + 1) * orow]
-            lse = jnp.where(lane == b, value, lse)
+        span = range(b0, b0 + together)
+        kept = []
+        for b in span:
+            landed(kv_v.at[b, 0, pl.ds(0, cached + fresh)], s_kv[b])
+            kept.append(score(cfg, b, len_s[b], tp, q_v, kv_v))
+        soft = [soften(cfg, k, scaling) for k in kept]
+        for b in span:
+            landed(kv_v.at[b, 1, pl.ds(0, cached + fresh)], s_vv[b])
         if b0 == 0:
             @pl.when(jnp.logical_not(leads))
             def _():
                 pl.semaphore_wait(barrier, n_tp - 1)
                 pl.semaphore_signal(news, inc=1, device_id=(rep, LEAD), device_id_type=MESH)
+        nums = [blend(cfg, soft[i][0], kv_v[b, 1]) for i, b in enumerate(span)]
+        for i, b in enumerate(span):
+            rounded, tops, total = soft[i]
+            out = (nums[i] / total).astype(jnp.bfloat16)
+            for t in range(n_tp):
+                send_o[t, b] = out[t * orow : (t + 1) * orow]
+            lse = jnp.where(lane == b, tops * scaling + jnp.log(total), lse)
     send_l[...] = lse.T[:TILE]
 
     @pl.when(leads)
@@ -225,10 +245,31 @@
     def _():
         pl.semaphore_wait(news, 1)
 
+    side = lax.rem(rep, 2)
+    across = 2 * line + 1 - side
+    relays = core == 1
+
+    def share(source, target, sem):
+        pltpu.make_async_remote_copy(
+            gathered.at[source], gathered.at[source], b_s, sem,
+            device_id=(target, tp), device_id_type=MESH).start()
+
+    def relay(p):
+        landed(gathered.at[p], z_r[p])
+        share(2 * p + side, across, b_r[p])
+
     for mask in far:
-        pltpu.make_async_remote_copy(
-            gathered.at[rep], gathered.at[rep], b_s, sems.at[first + rep // 2],
-            device_id=(flip(rep, mask, n_rep), tp), device_id_type=MESH).start()
+        there = flip(line, mask, pairs)
+        share(rep, 2 * there + side, sems.at[first + 2 * pairs + line])
+        if mask < half:
+            share(rep, 2 * there + 1 - side, sems.at[first + line])
+        else:
+            @pl.when(jnp.logical_not(relays & (line >= half)))
+            def _():
+                share(rep, 2 * there + 1 - side, sems.at[first + line])
+
+    share(rep, across, sems.at[first + line])
+
     partner = tp + 1 - 2 * core
 
     def keeper(p):
@@ -260,15 +301,21 @@
         for p in waiting:
             pass_on(p, distant)
         for p in batch_of:
-            mine = rep // 2 == p
-
-            @pl.when(mine)
+            if p == pairs - 1:
+                @pl.when(relays & (line < half))
+                def _():
+                    for q in range(pairs - 1, half - 1, -1):
+                        relay(q)
+
+            passed = line == p
+            if p >= half:
+                passed = passed | (relays & (line < half))
+
+            @pl.when(jnp.logical_not(passed))
             def _():
-                landed(gathered.at[0], b_r[p])
-
-            @pl.when(jnp.logical_not(mine))
-            def _():
-                landed(gathered.at[pl.ds(2 * p, 2)], b_r[p])
+                landed(gathered.at[2 * p], z_r[p])
+
+            landed(gathered.at[2 * p], b_r[p])
 
         block = jnp.concatenate([gathered[2 * p + i] for p in batch_of for i in range(2)], axis=0)
         proj = jnp.dot(block, w_v[...], preferred_element_type=jnp.float32).astype(jnp.bfloat16)
@@ -326,7 +373,16 @@
 
     landed(recv_l, al_s)
     landed(recv_o, ao_s)
-    landed(gathered.at[pl.ds(1, n_rep - 1)], b_s)
+    landed(gathered.at[pl.ds(0, n_rep - 1 - half)], b_s)
+
+    @pl.when(jnp.logical_not(relays & (line >= half)))
+    def _():
+        landed(gathered.at[pl.ds(0, half)], b_s)
+
+    @pl.when(relays & (line < half))
+    def _():
+        landed(gathered.at[pl.ds(0, half)], b_s)
+
     landed(other.at[pl.ds(0, half)], d_s)
     landed(sq_r.at[pl.ds(1, n_tp - 1)], q_s)
 
@@ -365,8 +421,9 @@
     vc = value_cache.reshape(batch, cached, hd)
     cfg = (n_rep, n_tp, batch, steps, heads, kv, block_len, own_w * n_tp, 1e-6)
     pairs = n_rep // 2
-    order = [[0], [1], [2, 3]] if pairs == 4 else [[p] for p in range(pairs)]
-    far = [m for p in range(pairs - 1, -1, -1) for m in (2 * p + 1, 2 * p) if m]
+    half = pairs // 2
+    order = [[0], [1], [3, 2]] if pairs == 4 else [[p] for p in [*range(half), *range(pairs - 1, half - 1, -1)]]
+    far = [*range(pairs - 1, 0, -1)]
     bf, f32 = jnp.bfloat16, jnp.float32
     anyspec = pl.BlockSpec(memory_space=pl.ANY)
     vmem = pl.BlockSpec(memory_space=pltpu.VMEM)
@@ -397,7 +454,7 @@
             pltpu.VMEM((batch, steps, own_w), bf),
             pltpu.VMEM((1, LANES), f32),
             pltpu.VMEM((n_tp, LANES), f32),
-            pltpu.SemaphoreType.DMA((LOADS + batch + SINGLES + 2 * pairs,)),
+            pltpu.SemaphoreType.DMA((LOADS + 2 * batch + SINGLES + 3 * pairs,)),
             pltpu.SemaphoreType.REGULAR,
         ],
         compiler_params=pltpu.CompilerParams(collective_id=0, has_side_effects=True),

time: 25.4 us -> 24.8 us (0.976)
  Pallas kernels: 23.7 us -> 23.3 us
    pallas_call x1, Pallas kernels: 23.7 us -> 23.3 us  [on_device(): pl.pallas_call(functools.partial(kernel, cfg, order, far), out_shape=(plt...]
where the time goes in v3:
time: 24.8 us; the launch traced here: 24.7 us
  Pallas kernels  23.3 us (94%)
  other arithmetic  0.7 us (3%)
  between operations  0.64 us (3%)
    pallas_call x1, Pallas kernels, on_device(): pl.pallas_call(functools.partial(kernel, cfg, order, far), out_shape=(plt...  23.3 us
    convert_element_type x1, other arithmetic, on_device(): return (hidden.astype(bf), (hidden * scale).astype(bf))  0.7 us

profile of v3, /device:TPU:0, one launch (start us, length us, event | category | flops | bytes accessed | tf_op | source)
XLA Modules:
  0.0 24.7 jit_solution(4779809763468634668)
XLA Ops:
  0.6 23.3 %shard_map.104 = (f32[4,4,2048]{2,1,0:T(4,128)S(1)}, f32[4,4,2048]{2,1,0:T(4,128)S(1)}) custom-call(s32[4]{0:T(128)} %len_hbm.1, bf16[4,128,128]{2,1,0:T(8,128)(2,1)} %bitcast.12, bf16[4,16,128]{2,1,0:T(8,128)(2,1)} %bitcast.13, bf16[4,16,128]{2,1,0:T(8,128)(2,1)} %bitcast.14, bf16[4,1024,128]{2,1,0:T(8,128)(2,1)} %bitcast.10, ...), custom_call_target="tpu_custom_call" | custom-call | tf_op jit(solution)/shard_map/pallas_call | solution.py:430
  24.0 0.7 %multiply_convert_fusion = (bf16[4,4,2048]{2,1,0:T(4,128)(2,1)}, bf16[4,4,2048]{2,1,0:T(4,128)(2,1)}) fusion(f32[4,4,2048]{2,1,0:T(4,128)S(1)} %get-tuple-element.4, f32[4,4,2048]{2,1,0:T(4,128)S(1)} %get-tuple-element.5), kind=kLoop, calls=%fused_computation | loop fusion | flops 98304 | bytes 393216 | tf_op jit(solution)/shard_map/convert_element_type | solution.py:462

commit v4 on v3

--- a/solution.py
+++ b/solution.py
@@ -117,8 +117,8 @@
 
     s_len, s_q, s_w, s_gain, s_x = (sems.at[i] for i in range(LOADS))
     s_kv = [sems.at[LOADS + b] for b in range(batch)]
-    s_vv = [sems.at[LOADS + batch + b] for b in range(batch)]
-    first = LOADS + 2 * batch
+    s_v = sems.at[LOADS + batch]
+    first = LOADS + batch + 1
     (ao_s, ao_r, al_s, al_r, b_s, d_s, c_s, c_r, q_s, q_r) = (
         sems.at[first + i] for i in range(SINGLES)
     )
@@ -128,15 +128,16 @@
     z_r = [sems.at[first + 2 * pairs + p] for p in range(pairs)]
 
     loads = [pltpu.make_async_copy(q_hbm, q_v, s_q)]
-    for b0 in range(0, batch, batch):
-        for i, old, new, marks in ((0, k_hbm, nk_hbm, s_kv), (1, v_hbm, nv_hbm, s_vv)):
-            for b in range(b0, b0 + batch):
-                loads += [
-                    pltpu.make_async_copy(old.at[b], kv_v.at[b, i, pl.ds(0, cached)], marks[b]),
-                    pltpu.make_async_copy(new.at[b], kv_v.at[b, i, pl.ds(cached, fresh)], marks[b]),
-                ]
-        if b0 == 0:
-            loads.append(pltpu.make_async_copy(len_hbm, len_s, s_len))
+    for b in range(batch):
+        loads += [
+            pltpu.make_async_copy(k_hbm.at[b], kv_v.at[b, 0, pl.ds(0, cached)], s_kv[b]),
+            pltpu.make_async_copy(nk_hbm.at[b], kv_v.at[b, 0, pl.ds(cached, fresh)], s_kv[b]),
+        ]
+    loads += [
+        pltpu.make_async_copy(len_hbm, len_s, s_len),
+        pltpu.make_async_copy(v_hbm, kv_v.at[:, 1, pl.ds(0, cached)], s_v),
+        pltpu.make_async_copy(nv_hbm, kv_v.at[:, 1, pl.ds(cached, fresh)], s_v),
+    ]
     loads += [
         pltpu.make_async_copy(w_hbm, w_v, s_w),
         pltpu.make_async_copy(gain_hbm, gain_v, s_gain),
@@ -182,8 +183,7 @@
             landed(kv_v.at[b, 0, pl.ds(0, cached + fresh)], s_kv[b])
             kept.append(score(cfg, b, len_s[b], tp, q_v, kv_v))
         soft = [soften(cfg, k, scaling) for k in kept]
-        for b in span:
-            landed(kv_v.at[b, 1, pl.ds(0, cached + fresh)], s_vv[b])
+        landed(kv_v.at[:, 1, pl.ds(0, cached + fresh)], s_v)
         if b0 == 0:
             @pl.when(jnp.logical_not(leads))
             def _():
@@ -202,12 +202,12 @@
     def _():
         pl.semaphore_wait(news, n_tp - 1)
 
-    for j in range(1, n_tp):
-        peer = lax.rem(tp + j, n_tp)
+    for mask in [*range(2, n_tp), 1]:
+        peer = flip(tp, mask, n_tp)
         pltpu.make_async_remote_copy(
-            send_l, recv_l.at[j - 1], al_s, al_r, device_id=(rep, peer), device_id_type=MESH).start()
+            send_l, recv_l.at[mask - 1], al_s, al_r, device_id=(rep, peer), device_id_type=MESH).start()
         pltpu.make_async_remote_copy(
-            send_o.at[peer], recv_o.at[j - 1], ao_s, ao_r, device_id=(rep, peer), device_id_type=MESH).start()
+            send_o.at[peer], recv_o.at[mask - 1], ao_s, ao_r, device_id=(rep, peer), device_id_type=MESH).start()
 
     @pl.when(leads)
     def _():
@@ -248,6 +248,7 @@
     side = lax.rem(rep, 2)
     across = 2 * line + 1 - side
     relays = core == 1
+    end = half // 2
 
     def share(source, target, sem):
         pltpu.make_async_remote_copy(
@@ -264,7 +265,7 @@
         if mask < half:
             share(rep, 2 * there + 1 - side, sems.at[first + line])
         else:
-            @pl.when(jnp.logical_not(relays & (line >= half)))
+            @pl.when(jnp.logical_not(relays & (line >= half) & (there < end)))
             def _():
                 share(rep, 2 * there + 1 - side, sems.at[first + line])
 
@@ -302,14 +303,14 @@
             pass_on(p, distant)
         for p in batch_of:
             if p == pairs - 1:
-                @pl.when(relays & (line < half))
+                @pl.when(relays & (line < end))
                 def _():
                     for q in range(pairs - 1, half - 1, -1):
                         relay(q)
 
             passed = line == p
             if p >= half:
-                passed = passed | (relays & (line < half))
+                passed = passed | (relays & (line < end))
 
             @pl.when(jnp.logical_not(passed))
             def _():
@@ -359,10 +360,10 @@
     hidden = x + jnp.concatenate(pieces, axis=1)
     squares = jnp.sum(hidden * hidden, axis=1, keepdims=True)
     sq_s[...] = jnp.sum(jnp.where(spot, squares, 0.0), axis=0, keepdims=True)
-    for j in range(1, n_tp):
+    for mask in [*range(2, n_tp), 1]:
         pltpu.make_async_remote_copy(
-            sq_s, sq_r.at[pl.ds(j, 1)], q_s, q_r,
-            device_id=(rep, lax.rem(tp + j, n_tp)), device_id_type=MESH).start()
+            sq_s, sq_r.at[pl.ds(mask, 1)], q_s, q_r,
+            device_id=(rep, flip(tp, mask, n_tp)), device_id_type=MESH).start()
     sq_r[0:1, :] = sq_s[...]
     hidden_ref[...] = hidden.reshape(hidden_ref.shape)
     landed(sq_r.at[pl.ds(1, n_tp - 1)], q_r)
@@ -373,13 +374,13 @@
 
     landed(recv_l, al_s)
     landed(recv_o, ao_s)
-    landed(gathered.at[pl.ds(0, n_rep - 1 - half)], b_s)
+    landed(gathered.at[pl.ds(0, n_rep - 1 - end)], b_s)
 
     @pl.when(jnp.logical_not(relays & (line >= half)))
     def _():
-        landed(gathered.at[pl.ds(0, half)], b_s)
-
-    @pl.when(relays & (line < half))
+        landed(gathered.at[pl.ds(0, end)], b_s)
+
+    @pl.when(relays & (line < end))
     def _():
         landed(gathered.at[pl.ds(0, half)], b_s)
 
@@ -406,7 +407,7 @@
     own_w = stream_in.shape[2]
     rows = batch * steps
     k_own = n_rep // n_tp
-    assert n_rep & (n_rep - 1) == 0
+    assert n_rep & (n_rep - 1) == 0 and n_tp & (n_tp - 1) == 0
     assert n_rep % n_tp == 0 and k_own % 2 == 0 and n_tp % 2 == 0 and heads % n_tp == 0
     assert batch <= TILE and k_own <= TILE and rows <= LANES and n_tp * TILE <= LANES
     owned = heads // n_tp
@@ -454,7 +455,7 @@
             pltpu.VMEM((batch, steps, own_w), bf),
             pltpu.VMEM((1, LANES), f32),
             pltpu.VMEM((n_tp, LANES), f32),
-            pltpu.SemaphoreType.DMA((LOADS + 2 * batch + SINGLES + 3 * pairs,)),
+            pltpu.SemaphoreType.DMA((LOADS + batch + 1 + SINGLES + 3 * pairs,)),
             pltpu.SemaphoreType.REGULAR,
         ],
         compiler_params=pltpu.CompilerParams(collective_id=0, has_side_effects=True),

time: 24.8 us -> 24.7 us (level)
  no operation moved by 1% of the time
where the time goes in v4:
time: 24.7 us; the launch traced here: 24.6 us
  Pallas kernels  23.2 us (94%)
  other arithmetic  0.7 us (3%)
  between operations  0.64 us (3%)
    pallas_call x1, Pallas kernels, on_device(): pl.pallas_call(functools.partial(kernel, cfg, order, far), out_shape=(plt...  23.2 us
    convert_element_type x1, other arithmetic, on_device(): return (hidden.astype(bf), (hidden * scale).astype(bf))  0.7 us

profile of v4, /device:TPU:0, one launch (start us, length us, event | category | flops | bytes accessed | tf_op | source)
XLA Modules:
  0.0 24.6 jit_solution(15578073914463886539)
XLA Ops:
  0.6 23.2 %shard_map.104 = (f32[4,4,2048]{2,1,0:T(4,128)S(1)}, f32[4,4,2048]{2,1,0:T(4,128)S(1)}) custom-call(s32[4]{0:T(128)} %len_hbm.1, bf16[4,128,128]{2,1,0:T(8,128)(2,1)} %bitcast.12, bf16[4,16,128]{2,1,0:T(8,128)(2,1)} %bitcast.13, bf16[4,16,128]{2,1,0:T(8,128)(2,1)} %bitcast.14, bf16[4,1024,128]{2,1,0:T(8,128)(2,1)} %bitcast.10, ...), custom_call_target="tpu_custom_call" | custom-call | tf_op jit(solution)/shard_map/pallas_call | solution.py:431
  23.9 0.7 %multiply_convert_fusion = (bf16[4,4,2048]{2,1,0:T(4,128)(2,1)}, bf16[4,4,2048]{2,1,0:T(4,128)(2,1)}) fusion(f32[4,4,2048]{2,1,0:T(4,128)S(1)} %get-tuple-element.4, f32[4,4,2048]{2,1,0:T(4,128)S(1)} %get-tuple-element.5), kind=kLoop, calls=%fused_computation | loop fusion | flops 98304 | bytes 393216 | tf_op jit(solution)/shard_map/convert_element_type | solution.py:463
